TPU v7x, 32 devices: a whole 2x2x4 slice. The times are simulated.
32 devices in a mesh: seq: 16 (over z, x, core), zero: 2 (over y).
Axes of the slice: x: 2, y: 2, z: 4, core: 2. Of those that a mesh axis runs over, the one named last changes fastest.
Arguments:
- tokens: bfloat16 [2, 2048, 2048], P('zero', 'seq'), may hold values from -6 to 6
- w_in: bfloat16 [2048, 2336], P('zero'), may hold values from -0.0625 to 0.0625
- a_log: float32 [32], replicated, may hold values from -8 to 0
- dt_bias: float32 [32], replicated, may hold values from -4.5 to -3.5
- d_skip: float32 [32], replicated, may hold values from 0.5 to 1.5
- grad_y: bfloat16 [2, 2048, 2048], P('zero', 'seq'), may hold values from -6 to 6
Outputs:
- y_out: bfloat16 [2, 2048, 2048], P('zero', 'seq')
- grad_tokens: bfloat16 [2, 2048, 2048], P('zero', 'seq')
- grad_w: float32 [2048, 2336], P(('seq', 'zero'))
All inputs are finite; a program needn't handle non-finite values.
Results may differ from a plain program's by a relative error of at most 0.013.
Values may be sent and summed in bfloat16 or wider, within the bound.
A program may use at most 128 MiB of HBM per device.

v0:
```python
import functools

import jax
import jax.numpy as jnp
from jax import lax
from jax.experimental import pallas as pl
from jax.experimental.pallas import tpu as pltpu
from jax.sharding import PartitionSpec as P

BF = jnp.bfloat16
F32 = jnp.float32
MESH = pl.DeviceIdType.MESH
LAGS = (0, 1, 3, 5, 6)
SPACING = (3, 3)
SWAPPED = (0, 5)


def dot(a, b, dims):
    return lax.dot_general(a, b, (dims, ((), ())), preferred_element_type=F32)


def greet(peers, mates=()):
    barrier = pltpu.get_barrier_semaphore()
    for peer in peers:
        pl.semaphore_signal(barrier, inc=1, device_id={"seq": peer}, device_id_type=MESH)
    for mate in mates:
        pl.semaphore_signal(barrier, inc=1, device_id={"zero": mate}, device_id_type=MESH)
    pl.semaphore_wait(barrier, len(peers) + len(mates))


def remote(src, dst, send, recv, peer):
    return pltpu.make_async_remote_copy(
        src_ref=src,
        dst_ref=dst,
        send_sem=send,
        recv_sem=recv,
        device_id={"seq": peer},
        device_id_type=MESH,
    )


def mate(src, dst, send, recv, peer):
    return pltpu.make_async_remote_copy(
        src_ref=src,
        dst_ref=dst,
        send_sem=send,
        recv_sem=recv,
        device_id={"zero": peer},
        device_id_type=MESH,
    )


def head_kernel(
    zero, inner, rows, stored, xs, pair, raw, weights, guest, kept, made, narrow, back, thin,
    send, recv, load
):
    here = lax.axis_index("zero")
    columns, owned = weights.shape
    exact = made.shape[2]
    heads = columns - exact
    after = [lax.rem(here + s, zero) for s in range(zero)]
    before = [lax.rem(here + zero - s, zero) for s in range(zero)]
    fetch = pltpu.make_async_copy(stored, weights, load)
    fetch.start()
    greet([], after[1:])

    def columns_of(z):
        return pl.ds(pl.multiple_of(z * owned, 128), owned)

    coming = []
    for s in range(1, zero):
        copy = mate(rows.at[:, columns_of(after[s])], guest.at[s - 1], send.at[s, 0], recv.at[s, 0], after[s])
        copy.start()
        coming.append(copy)
    edges = list(range(0, inner, 256)) + [inner]
    spans = [(inner, exact)] + list(zip(edges[:-1], edges[1:]))
    fetch.wait()
    mine = rows[:, columns_of(here)]
    for low, high in spans + [(exact, columns)]:
        kept[:, low:high] = dot(mine, weights[low:high], ((1,), (1,)))
    going = {}
    narrow[...] = jnp.zeros(narrow.shape, F32)
    for s in range(1, zero):
        coming[s - 1].wait()
        narrow[s - 1, :, :heads] = dot(guest[s - 1], weights[exact:], ((1,), (1,)))
        copy = mate(narrow.at[s - 1], thin.at[s - 1], send.at[s, 1], recv.at[s, 1], before[s])
        copy.start()
        going[s, -1] = copy
        for i, (low, high) in enumerate(spans):
            value = dot(guest[s - 1], weights[low:high], ((1,), (1,)))
            made[s - 1, :, low:high] = value.astype(BF)
            copy = mate(
                made.at[s - 1, :, low:high],
                back.at[s - 1, :, low:high],
                send.at[s, 2 + i],
                recv.at[s, 2 + i],
                before[s],
            )
            copy.start()
            going[s, i] = copy
    total = kept[:, exact:]
    for s in range(1, zero):
        going[s, -1].wait()
        total = total + thin[s - 1, :, :heads]
    raw[...] = total
    for i, (low, high) in enumerate(spans):
        total = kept[:, low:high]
        for s in range(1, zero):
            going[s, i].wait()
            total = total + back[s - 1, :, low:high].astype(F32)
        if i:
            xs[:, low:high] = total.astype(BF)
        else:
            pair[...] = total.astype(BF)


def head(rows, weights, inner, heads):
    count, width = rows.shape
    columns, owned = weights.shape
    zero = width // owned
    exact = columns - heads
    steps = 3 + -(-inner // 256)
    return pl.pallas_call(
        functools.partial(head_kernel, zero, inner),
        out_shape=(
            jax.ShapeDtypeStruct((count, inner), BF),
            jax.ShapeDtypeStruct((count, exact - inner), BF),
            jax.ShapeDtypeStruct((count, heads), F32),
        ),
        in_specs=[pl.BlockSpec(memory_space=pltpu.VMEM), pl.BlockSpec(memory_space=pl.ANY)],
        out_specs=[pl.BlockSpec(memory_space=pltpu.VMEM)] * 3,
        scratch_shapes=[
            pltpu.VMEM((columns, owned), BF),
            pltpu.VMEM((zero - 1, count, owned), BF),
            pltpu.VMEM((count, columns), F32),
            pltpu.VMEM((zero - 1, count, exact), BF),
            pltpu.VMEM((zero - 1, count, 128), F32),
            pltpu.VMEM((zero - 1, count, exact), BF),
            pltpu.VMEM((zero - 1, count, 128), F32),
            pltpu.SemaphoreType.DMA((zero, steps)),
            pltpu.SemaphoreType.DMA((zero, steps)),
            pltpu.SemaphoreType.DMA,
        ],
        compiler_params=pltpu.CompilerParams(collective_id=2, vmem_limit_bytes=14 << 20, has_side_effects=True),
    )(rows, weights)


def core_kernel(
    width, chunk, lags, spans, tile,
    xs, joined, raws, gy, rows, stored, a_log, dt_bias, d_skip, y_out, out, grads,
    spread, dts, grows, fades, xds, growns, fadeds, ins, backs, cums, turned, mark, marks, gains,
    loc, both, pairs, duo, sums, far, ret, came, fin, wide, tall, left, right, weights, made,
    tsend, trecv, send, recv, zsend, zrecv, leave, enter, *scratch
):
    seq, planes = marks.shape[0], far.shape[2]
    zero = tall.shape[2]
    load = pltpu.make_async_copy(stored, weights, scratch[-1])
    load.start()
    me, here = lax.axis_index("seq"), lax.axis_index("zero")
    core, chip = lax.rem(me, 2), lax.div(me, 2)
    side, plane = lax.rem(chip, 2), lax.div(chip, 2)
    sibling, across = me + 1 - 2 * core, me + 2 - 4 * side
    peers = [lax.rem(me + d, seq) for d in range(1, seq)]
    after = [lax.rem(here + s, zero) for s in range(zero)]
    before = [lax.rem(here + zero - s, zero) for s in range(zero)]
    count, inner = xs.shape
    heads = raws.shape[1]
    size = joined.shape[1] // 2
    chunks = inner // chunk
    high = lax.Precision.HIGHEST
    far[...] = jnp.zeros(far.shape, BF)
    mark[...] = jnp.zeros(mark.shape, F32)
    greet(peers, after[1:])
    def iota(shape, axis):
        return lax.broadcasted_iota(jnp.int32, shape, axis)

    lower = iota((count, count), 0) >= iota((count, count), 1)
    ones = lower.astype(F32)
    first = iota((heads, inner), 0) * width
    lane = iota((heads, inner), 1)
    spread[...] = ((lane >= first) & (lane < first + width)).astype(F32)
    rate, skip = -jnp.exp(a_log[...]), d_skip[...]
    raw = raws[...] + dt_bias[...]
    dt = jnp.maximum(raw, 0.0) + jnp.log1p(jnp.exp(-jnp.abs(raw)))
    cum = jnp.dot(ones, rate * dt, precision=high, preferred_element_type=F32)
    total = cum[count - 1 : count]
    cums[...] = cum
    turned[...] = cum.T
    mark[0:1, :heads] = total
    marks[me] = mark[...]
    told = [
        remote(mark, marks.at[me], tsend.at[d], trecv.at[d], peer) for d, peer in enumerate(peers)
    ]
    for copy in told:
        copy.start()
    growth, fade = jnp.exp(cum), jnp.exp(total - cum)
    bm, cm = joined[:, :size], joined[:, size:]
    bt, ct = bm.T, cm.T
    skips = jnp.broadcast_to(skip, (8, heads))

    def expand(value, low, top):
        return jnp.dot(value, spread[:, low:top], precision=high, preferred_element_type=F32)

    def gather(value, low, top):
        return lax.dot_general(
            value, spread[:, low:top], (((1,), (1,)), ((), ())), precision=high,
            preferred_element_type=F32,
        )

    step = min(256, chunk)
    copies = {}

    def prepare(c):
        for low in range(c * chunk, (c + 1) * chunk, step):
            top = low + step
            own = slice(low - c * chunk, low - c * chunk + step)
            d, g, f = expand(dt, low, top), expand(growth, low, top), expand(fade, low, top)
            dts[:, low:top], grows[:, low:top], fades[:, low:top] = d, g, f
            xd = (xs[:, low:top].astype(F32) * d).astype(BF)
            grown = (gy[:, low:top].astype(F32) * g).astype(BF)
            faded = (xd.astype(F32) * f).astype(BF)
            xds[:, low:top], growns[:, low:top], fadeds[:, low:top] = xd, grown, faded
            parts = loc.shape[1:2] + loc.shape[3:5] + (step,)
            loc[c, :, 0, :, :, own] = dot(bt, faded, ((1,), (0,))).astype(BF).reshape(parts)
            loc[c, :, 1, :, :, own] = dot(ct, grown, ((1,), (0,))).astype(BF).reshape(parts)
        both[c, core] = loc[c, core]
        copies[0, c] = remote(
            loc.at[c, 1 - core], both.at[c, core], send.at[0, c], recv.at[0, c], sibling
        )
        copies[0, c].start()

    def gain(c, *rows):
        at = slice(c * chunk, (c + 1) * chunk)
        return jnp.exp(sum(gains[pl.ds(row, 1), at] for row in rows))

    def stage_pair(c):
        copies[0, c].wait()
        g0, g1 = gain(c, chip * 2), gain(c, chip * 2 + 1)
        for q in range(2):
            pairs[c, q, 0] = (
                g1 * both[c, 0, 0, q].astype(F32) + both[c, 1, 0, q].astype(F32)
            ).astype(BF)
            pairs[c, q, 1] = (
                g0 * both[c, 1, 1, q].astype(F32) + both[c, 0, 1, q].astype(F32)
            ).astype(BF)
        duo[c, side] = pairs[c, side]
        copies[1, c] = remote(
            pairs.at[c, 1 - side], duo.at[c, side], send.at[1, c], recv.at[1, c], across
        )
        copies[1, c].start()

    def along(c, way, d):
        return remote(
            sums.at[c, way],
            far.at[c, way, plane],
            zsend.at[c, way, d],
            zrecv.at[c, way, d],
            me + (4 * d if way == 0 else -4 * d),
        )

    def later(d, way):
        return plane + d < planes if way == 0 else plane >= d

    def stage_plane(c):
        copies[1, c].wait()
        g0 = gain(c, plane * 4, plane * 4 + 1)
        g1 = gain(c, plane * 4 + 2, plane * 4 + 3)
        sums[c, 0] = (g1 * duo[c, 0, 0].astype(F32) + duo[c, 1, 0].astype(F32)).astype(BF)
        sums[c, 1] = (g0 * duo[c, 1, 1].astype(F32) + duo[c, 0, 1].astype(F32)).astype(BF)
        for d in range(1, planes):
            for way in range(2):

                @pl.when(later(d, way))
                def _():
                    along(c, way, d).start()

    def stage_far(c):
        for d in range(1, planes):
            for way in range(2):

                @pl.when(later(d, 1 - way))
                def _():
                    along(c, way, d).wait_recv()

                @pl.when(later(d, way))
                def _():
                    along(c, way, d).wait_send()

        at = slice(c * chunk, (c + 1) * chunk)
        ends = []
        for way in range(2):
            run = jnp.zeros(far.shape[3:], F32)
            for k in range(planes) if way == 0 else reversed(range(planes)):
                inside = (k < plane if way == 0 else k > plane).astype(F32)
                whole = sum(gains[4 * k + i : 4 * k + i + 1, at] for i in range(4))
                run = jnp.exp(whole * inside) * run + far[c, way, k].astype(F32)
            ends.append(run)
        g0 = gain(c, plane * 4, plane * 4 + 1)
        g1 = gain(c, plane * 4 + 2, plane * 4 + 3)
        ret[c, 0, 0] = ends[0].astype(BF)
        ret[c, 1, 0] = (g0 * ends[0] + duo[c, 0, 0].astype(F32)).astype(BF)
        ret[c, 1, 1] = ends[1].astype(BF)
        ret[c, 0, 1] = (g1 * ends[1] + duo[c, 1, 1].astype(F32)).astype(BF)
        came[c, side] = ret[c, side]
        copies[2, c] = remote(
            ret.at[c, 1 - side], came.at[c, side], send.at[2, c], recv.at[2, c], across
        )
        copies[2, c].start()

    def stage_back(c):
        copies[2, c].wait()
        g0, g1 = gain(c, chip * 2), gain(c, chip * 2 + 1)
        for q in range(2):
            fin[c, 0, 0, q] = came[c, q, 0]
            fin[c, 1, 1, q] = came[c, q, 1]
            fin[c, 1, 0, q] = (
                g0 * came[c, q, 0].astype(F32) + both[c, 0, 0, q].astype(F32)
            ).astype(BF)
            fin[c, 0, 1, q] = (
                g1 * came[c, q, 1].astype(F32) + both[c, 1, 1, q].astype(F32)
            ).astype(BF)
        wide[c, core] = fin[c, core]
        copies[3, c] = remote(
            fin.at[c, 1 - core], wide.at[c, core], send.at[3, c], recv.at[3, c], sibling
        )
        copies[3, c].start()

    scores = dot(cm, bm, ((1,), (1,)))
    group = 128 // width
    state = {
        "mixed": jnp.zeros((count, count), F32),
        "c": jnp.zeros((count, size), F32),
        "b": jnp.zeros((count, size), F32),
        "log": jnp.zeros((count, heads), F32),
        "dt": jnp.zeros((count, heads), F32),
        "last": jnp.zeros((8, heads), F32),
    }
    place = iota((count, 128), 1)
    masks = [(place >= width * i) & (place < width * (i + 1)) for i in range(group)]

    def inside(p):
        low, top = p * 128, (p + 1) * 128
        x2, g2 = xds[:, low:top], gy[:, low:top]
        none = jnp.zeros_like(x2)
        decays = []
        for i in range(group):
            h = p * group + i
            spans = cums[:, h : h + 1] - turned[h : h + 1, :]
            decays.append(jnp.where(lower, jnp.exp(jnp.where(lower, spans, 0.0)), 0.0))
        mixing = jnp.concatenate([(scores * decay).astype(BF) for decay in decays], axis=1)
        stacked = jnp.concatenate([jnp.where(mask, x2, none) for mask in masks], axis=0)
        ins[:, low:top] = dot(mixing, stacked, ((1,), (0,)))
        tall = dot(mixing, g2, ((0,), (0,)))
        back = tall[:count]
        for i in range(1, group):
            back = jnp.where(masks[i], tall[i * count : (i + 1) * count], back)
        backs[:, low:top] = back
        lifted = jnp.concatenate([jnp.where(mask, g2, none) for mask in masks], axis=0)
        cross = dot(lifted, x2, ((1,), (1,)))
        for i in range(group):
            state["mixed"] += cross[i * count : (i + 1) * count] * decays[i]

    def finish(c):
        copies[3, c].wait()
        for low in range(c * chunk, (c + 1) * chunk, step):
            top = low + step
            own = slice(low - c * chunk, low - c * chunk + step)
            start = wide[c, :, 0, :, :, own].reshape(size, step)
            end = wide[c, :, 1, :, :, own].reshape(size, step)
            x, g = xs[:, low:top].astype(F32), gy[:, low:top].astype(F32)
            d, xd = dts[:, low:top], xds[:, low:top].astype(F32)
            reached = dot(bm, end, ((1,), (0,))) * fades[:, low:top]
            y3 = ins[:, low:top] + dot(cm, start, ((1,), (0,))) * grows[:, low:top]
            h3 = backs[:, low:top] + reached
            kept = expand(skips, low, top)[:1]
            y_out[:, low:top] = (y3 + kept * x).astype(BF)
            right[:count, low:top] = (h3 * d + kept * g).astype(BF)
            state["c"] += dot(growns[:, low:top], start, ((1,), (1,)))
            state["b"] += dot(fadeds[:, low:top], end, ((1,), (1,)))
            state["log"] += gather(g * y3 - xd * h3, low, top)
            state["dt"] += gather(x * h3, low, top)
            joint = jnp.sum(start.astype(F32) * end.astype(F32), axis=0, keepdims=True)
            joint = joint * jnp.exp(gains[pl.ds(me, 1), low:top])
            last = jnp.sum(xd * reached, axis=0, keepdims=True) + joint
            state["last"] += gather(jnp.broadcast_to(last, (8, step)), low, top)

    pieces, piece, tokens = left.shape[1:]
    levels = (seq // 2).bit_length() - 1
    bits = [lax.rem(lax.div(chip, 1 << b), 2) for b in range(levels)]
    partners = [me + (1 - 2 * bits[b]) * (2 << b) for b in range(levels)]
    parts = len(spans)
    up = list(range(levels))
    orders = [up[1:] + up[:1] if h in SWAPPED else up for h in range(parts)]
    acc, away, come = (scratch[i * parts : (i + 1) * parts] for i in range(3))
    rest = scratch[3 * parts : -7]
    outs = [rest[h * levels : (h + 1) * levels] for h in range(parts)]
    inns = [rest[(parts + h) * levels : (parts + h + 1) * levels] for h in range(parts)]
    dsend, drecv, put, got, back_send, back_recv = scratch[-7:-1]
    crossing = []

    def cross():
        for low in range(0, rows.shape[1], 128):
            block = rows[:, low : low + 128].astype(F32).T.reshape(128 // piece, piece, count)
            for i in range(128 // piece):
                q = low // piece + i
                tall[q // (2 * zero), q // zero % 2, q % zero] = block[i].astype(BF)
        for way in range(2):
            for s in range(1, zero):
                copy = mate(
                    tall.at[:, way, after[s]],
                    left.at[way, :, :, s * count : (s + 1) * count],
                    leave.at[way, s - 1],
                    enter.at[way, s - 1],
                    after[s],
                )
                copy.start()
                crossing.append(copy)
            left[way, :, :, :count] = tall[:, way, here]

    arriving = {}

    def ready(h):
        low, high = spans[h]
        arriving[h] = []
        for s in range(1, zero):
            copy = mate(
                right.at[:count, low:high],
                right.at[s * count : (s + 1) * count, low:high],
                put.at[h, s],
                got.at[h, s],
                after[s],
            )
            copy.start()
            arriving[h].append(copy)

    columns, owned = weights.shape
    mine_at = pl.multiple_of(here * owned, 128)

    def project(values, target, origin):
        @pl.loop(0, owned // tile)
        def _(i):
            at = pl.multiple_of(i * tile, 128)
            value = dot(values[:, :columns], weights[:, pl.ds(at, tile)], ((1,), (0,)))
            target[:, pl.ds(pl.multiple_of(origin + at, 128), tile)] = value.astype(BF)


    def multiply(side, h, target):
        low, high = spans[h]
        lines = left[side].reshape(pieces * piece, tokens)
        value = jnp.dot(lines, right[:, low:high], preferred_element_type=F32)
        target[...] = value.reshape(target.shape).astype(target.dtype)

    pushed = []

    def front(h):
        for copy in arriving[h]:
            copy.wait()
        multiply(1 - core, h, away[h])
        copy = remote(away[h], come[h], dsend.at[h, levels], drecv.at[h, levels], sibling)
        copy.start()
        pushed.append(copy)
        multiply(core, h, acc[h])

    def join(h):
        pushed[h].wait()

        @pl.loop(0, pieces)
        def _(i):
            acc[h][i] += come[h][i].astype(F32)

    def subsets(rest):
        found = [0]
        for b in rest:
            found = found + [value + (1 << b) for value in found]
        return found

    flying = {}

    def begin(h, s):
        order = orders[h]
        b = order[s]
        base = sum((bits[f] * (1 << f) for f in order[:s]), 0)
        for j, extra in enumerate(subsets(order[s + 1 :])):
            outs[h][s][j] = acc[h][base + (1 - bits[b]) * (1 << b) + extra].astype(BF)
        copy = remote(outs[h][s], inns[h][s], dsend.at[h, s], drecv.at[h, s], partners[b])
        copy.start()
        flying[h] = copy

    def settle(h, s):
        flying[h].wait()
        order = orders[h]
        base = sum((bits[f] * (1 << f) for f in order[: s + 1]), 0)
        for j, extra in enumerate(subsets(order[s + 1 :])):
            acc[h][base + extra] += inns[h][s][j].astype(F32)

    lag, skew = SPACING
    returning = []

    def advance(k):
        if k < parts:
            front(k)
        if 1 <= k <= parts:
            join(k - 1)
            begin(k - 1, 0)
        if k == parts:
            load.wait()
            for s in range(1, zero):
                project(right.at[s * count : (s + 1) * count], made.at[s - 1], 0)
                copy = mate(
                    made.at[s - 1],
                    grads.at[:, pl.ds(mine_at, owned)],
                    back_send.at[s],
                    back_recv.at[s],
                    before[s],
                )
                copy.start()
                returning.append(copy)
            project(right.at[:count], grads, mine_at)
        for s in reversed(range(levels)):
            h = k - lag - skew * s
            if 0 <= h < parts:
                settle(h, s)
                if s + 1 < levels:
                    begin(h, s + 1)
                else:
                    low, high = spans[h][0], min(spans[h][1], columns)
                    out[:, low:high] = acc[h][chip, :, : high - low]

    for c in range(chunks):
        prepare(c)
    for copy in told:
        copy.wait()
    totals = marks[:, 0, :heads]
    for low in range(0, inner, step):
        gains[:, low : low + step] = expand(totals, low, low + step)
    stages = [stage_pair, stage_plane, stage_far, stage_back, finish]
    steps = chunks + lags[-1]
    fillers = list(range(inner // 128))
    per = -(-len(fillers) // lags[-1])
    moved = 0
    for k in range(steps):
        for lagging, stage in reversed(list(zip(lags, stages))):
            c = k - lagging
            if 0 <= c < chunks:
                if stage is finish:
                    while fillers and fillers[0] * 128 < (c + 1) * chunk:
                        inside(fillers.pop(0))
                stage(c)
                if stage is finish:
                    for h in range(parts):
                        if c * chunk <= spans[h][0] < (c + 1) * chunk:
                            ready(h)
        if k == 0:
            cross()
        for _ in range(per):
            if fillers:
                inside(fillers.pop(0))
        if k == lags[-1] + 1:
            for copy in crossing:
                copy.wait()
        if k > lags[-1]:
            while spans[moved][0] < (k - lags[-1]) * chunk:
                advance(moved)
                moved += 1

    mixed = state["mixed"].astype(BF)
    right[:count, inner : inner + size] = (dot(mixed, cm, ((0,), (0,))) + state["b"]).astype(BF)
    right[:count, inner + size : inner + 2 * size] = (
        dot(mixed, bm, ((1,), (0,))) + state["c"]
    ).astype(BF)
    upper = (iota((count, count), 0) <= iota((count, count), 1)).astype(F32)
    grad_log = jnp.dot(upper, state["log"], precision=high, preferred_element_type=F32)
    grad_log = grad_log + state["last"][:1]
    grad_raw = (state["dt"] + grad_log * rate) * jax.nn.sigmoid(raw)
    edge = inner + 2 * size
    right[:count, edge:] = jnp.zeros((count, right.shape[1] - edge), BF)
    right[:count, edge : edge + heads] = grad_raw.astype(BF)
    for h in range(parts):
        if spans[h][0] >= inner:
            ready(h)
    for k in range(moved, parts + lag + skew * levels):
        advance(k)
    for copy in returning:
        copy.wait()


def ssd_block(xs, joined, raw, gy, rows, weights, a_log, dt_bias, d_skip):
    count, inner = gy.shape
    heads = a_log.shape[0]
    size = joined.shape[1] // 2
    columns, owned = weights.shape
    seq, zero = lax.axis_size("seq"), lax.axis_size("zero")
    planes, pieces = seq // 4, seq // 2
    piece, tokens = owned // seq, zero * count
    levels = pieces.bit_length() - 1
    chunk = 512
    chunks = inner // chunk
    quarter = size // 4
    padded = -(-columns // 128) * 128
    edges = list(range(0, padded, 256)) + [padded]
    spans = list(zip(edges[:-1], edges[1:]))
    parts = len(spans)
    widths = [high - low for low, high in spans]
    tall = pltpu.VMEM((count, inner), F32)
    thin = pltpu.VMEM((count, inner), BF)
    block = pltpu.VMEM((chunks, 2, 2, 2, quarter, chunk), BF)
    half = pltpu.VMEM((chunks, 2, 2, quarter, chunk), BF)
    dma = pltpu.SemaphoreType.DMA
    scratch = [
        pltpu.VMEM((heads, inner), F32),
        tall, tall, tall, thin, thin, thin, tall, tall,
        pltpu.VMEM((count, heads), F32),
        pltpu.VMEM((heads, count), F32),
        pltpu.VMEM((8, 128), F32),
        pltpu.VMEM((seq, 8, 128), F32),
        pltpu.VMEM((seq, inner), F32),
        block, block, half, half,
        pltpu.VMEM((chunks, 2, quarter, chunk), BF),
        pltpu.VMEM((chunks, 2, planes, quarter, chunk), BF),
        half, half, block, block,
        pltpu.VMEM((pieces, 2, zero, piece, count), BF),
        pltpu.VMEM((2, pieces, piece, tokens), BF),
        pltpu.VMEM((tokens, padded), BF),
        pltpu.VMEM(weights.shape, BF),
        pltpu.VMEM((zero - 1, count, owned), BF),
        dma((seq - 1,)), dma((seq - 1,)),
        dma((4, chunks)), dma((4, chunks)),
        dma((chunks, 2, planes)), dma((chunks, 2, planes)),
        dma((2, zero - 1)), dma((2, zero - 1)),
    ]
    scratch += [pltpu.VMEM((pieces, piece, w), F32) for w in widths]
    scratch += [pltpu.VMEM((pieces, piece, w), BF) for w in widths] * 2
    for _ in range(2):
        for w in widths:
            scratch += [pltpu.VMEM((pieces >> (s + 1), piece, w), BF) for s in range(levels)]
    scratch += [dma((parts, levels + 1))] * 2 + [dma((parts, zero))] * 2 + [dma((zero,))] * 2
    scratch += [dma]
    local = pl.BlockSpec(memory_space=pltpu.VMEM)
    return pl.pallas_call(
        functools.partial(core_kernel, inner // heads, chunk, LAGS, spans, min(256, owned)),
        out_shape=(
            jax.ShapeDtypeStruct((count, inner), BF),
            jax.ShapeDtypeStruct((piece, columns), F32),
            jax.ShapeDtypeStruct((count, zero * owned), BF),
        ),
        in_specs=[local] * 5 + [pl.BlockSpec(memory_space=pl.ANY)] + [local] * 3,
        out_specs=[local] * 3,
        scratch_shapes=scratch,
        compiler_params=pltpu.CompilerParams(collective_id=0, vmem_limit_bytes=48 << 20, has_side_effects=True),
    )(xs, joined, raw, gy, rows, weights, a_log[None], dt_bias[None], d_skip[None])


def per_device(tokens, w_in, a_log, dt_bias, d_skip, grad_y):
    count, width = tokens.shape[1:]
    inner = grad_y.shape[2]
    heads = a_log.shape[0]
    rows = tokens.reshape(count, width)

    stored = w_in.T
    xs, joined, raw = head(rows, stored, inner, heads)

    y_out, grad_w, grad_tokens = ssd_block(
        xs, joined, raw, grad_y.reshape(count, inner), rows, stored, a_log, dt_bias, d_skip
    )
    grad_tokens = grad_tokens.reshape(1, count, width)
    return (y_out.reshape(1, count, inner), grad_tokens, grad_w)


def solution(mesh):
    placed = (P("zero", "seq", None), P("zero", None), P(), P(), P(), P("zero", "seq", None))
    return jax.shard_map(
        per_device,
        mesh=mesh,
        in_specs=placed,
        out_specs=(P("zero", "seq", None), P("zero", "seq", None), P(("seq", "zero"), None)),
        check_vma=False,
    )
```

profile of v0, /device:TPU:0, one launch (start us, length us, event | category | flops | bytes accessed | tf_op | source)
XLA Modules:
  0.0 100.2 jit_solution(2156322715531045070)
XLA Ops:
  0.6 0.0 copy-start.6
  0.6 0.0 copy-start.5
  0.7 0.0 copy-start.4
  0.7 0.0 copy-start
  0.7 2.4 %copy-done = bf16[1024,2336]{0,1:T(8,128)(2,1)S(1)} copy-done((bf16[1024,2336]{0,1:T(8,128)(2,1)S(1)}, bf16[1024,2336]{0,1:T(8,128)(2,1)}, u32[]{:S(2)}) %copy-start) | copy-done | bytes 4784152
  3.0 0.0 copy-start.1
  3.0 1.0 %copy-done.1 = bf16[1,128,2048]{2,1,0:T(8,128)(2,1)S(1)} copy-done((bf16[1,128,2048]{2,1,0:T(8,128)(2,1)S(1)}, bf16[1,128,2048]{2,1,0:T(8,128)(2,1)}, u32[]{:S(2)}) %copy-start.1) | copy-done | bytes 524312
  4.1 0.0 copy-start.2
  4.1 0.0 copy-start.3
  4.1 26.0 %shard_map.85 = (bf16[128,2048]{1,0:T(8,128)(2,1)S(1)}, bf16[128,256]{1,0:T(8,128)(2,1)S(1)}, f32[128,32]{1,0:T(8,128)S(1)}) custom-call(bf16[128,2048]{1,0:T(8,128)(2,1)S(1)} %bitcast.10, bf16[2336,1024]{1,0:T(8,128)(2,1)S(1)} %bitcast.9), custom_call_target="tpu_custom_call" | custom-call | tf_op jit(solution)/shard_map/pallas_call | solution.py:123
  30.1 0.0 copy-done.6
  30.1 0.0 copy-done.5
  30.1 0.0 copy-done.4
  30.1 0.0 copy-done.2
  30.1 0.0 copy-done.3
  30.1 67.7 %shard_map.86 = (bf16[128,2048]{1,0:T(8,128)(2,1)S(1)}, f32[64,2336]{1,0:T(8,128)S(1)}, bf16[128,2048]{1,0:T(8,128)(2,1)S(1)}) custom-call(bf16[128,2048]{1,0:T(8,128)(2,1)S(1)} %get-tuple-element.9.xs, bf16[128,256]{1,0:T(8,128)(2,1)S(1)} %get-tuple-element.10.joined, f32[128,32]{1,0:T(8,128)S(1)} %get-tuple-element.11.raws, ...), custom_call_target="tpu_custom_call" | custom-call | tf_op jit(solution)/shard_map/pallas_call | solution.py:639
  97.8 0.8 copy.12
  98.6 0.8 copy.13
  99.4 0.8 copy.14
Async XLA Ops:
  0.6 29.5 %copy-start.6 = (f32[32]{0:T(128)S(1)}, f32[32]{0:T(128)}, u32[]{:S(2)}) copy-start(f32[32]{0:T(128)} %param.10) | copy-start | bytes 388
  0.6 29.5 %copy-start.5 = (f32[32]{0:T(128)S(1)}, f32[32]{0:T(128)}, u32[]{:S(2)}) copy-start(f32[32]{0:T(128)} %param.9) | copy-start | bytes 388
  0.7 29.5 %copy-start.4 = (f32[32]{0:T(128)S(1)}, f32[32]{0:T(128)}, u32[]{:S(2)}) copy-start(f32[32]{0:T(128)} %param.8) | copy-start | bytes 388
  0.7 2.4 %copy-start = (bf16[1024,2336]{0,1:T(8,128)(2,1)S(1)}, bf16[1024,2336]{0,1:T(8,128)(2,1)}, u32[]{:S(2)}) copy-start(bf16[1024,2336]{0,1:T(8,128)(2,1)} %param.7) | copy-start | bytes 14352388
  3.0 1.0 %copy-start.1 = (bf16[1,128,2048]{2,1,0:T(8,128)(2,1)S(1)}, bf16[1,128,2048]{2,1,0:T(8,128)(2,1)}, u32[]{:S(2)}) copy-start(bf16[1,128,2048]{2,1,0:T(8,128)(2,1)} %param.6) | copy-start | bytes 1572868
  4.1 26.0 %copy-start.2 = (bf16[1,128,2048]{2,1,0:T(8,128)(2,1)S(1)}, bf16[1,128,2048]{2,1,0:T(8,128)(2,1)}, u32[]{:S(2)}) copy-start(bf16[1,128,2048]{2,1,0:T(8,128)(2,1)} %param.6) | copy-start | bytes 1572868
  4.1 26.0 %copy-start.3 = (bf16[1,128,2048]{2,1,0:T(8,128)(2,1)S(1)}, bf16[1,128,2048]{2,1,0:T(8,128)(2,1)}, u32[]{:S(2)}) copy-start(bf16[1,128,2048]{2,1,0:T(8,128)(2,1)} %param.11) | copy-start | bytes 1572868
where the time goes:
time: 100 us
  Pallas kernels  93.7 us (94%)
  local copies, waits for them, and re-layouts  5.84 us (6%)
    pallas_call x1, Pallas kernels, ssd_block(): pl.pallas_call(functools.partial(core_kernel, inner // heads, chunk, LAGS...  67.7 us
    pallas_call x1, Pallas kernels, head(): pl.pallas_call(functools.partial(head_kernel, zero, inner), out_shape=(ja...  26 us
    unnamed x17, local copies, waits for them, and re-layouts  5.84 us

commit v1 on v0

--- a/solution.py
+++ b/solution.py
@@ -8,9 +8,10 @@
 from jax.sharding import PartitionSpec as P
 
 BF = jnp.bfloat16
+VMEM = 56 << 20
 F32 = jnp.float32
 MESH = pl.DeviceIdType.MESH
-LAGS = (0, 1, 3, 5, 6)
+LAGS = (0, 1, 2, 4, 5, 6)
 SPACING = (3, 3)
 SWAPPED = (0, 5)
 
@@ -50,105 +51,10 @@
     )
 
 
-def head_kernel(
-    zero, inner, rows, stored, xs, pair, raw, weights, guest, kept, made, narrow, back, thin,
-    send, recv, load
-):
-    here = lax.axis_index("zero")
-    columns, owned = weights.shape
-    exact = made.shape[2]
-    heads = columns - exact
-    after = [lax.rem(here + s, zero) for s in range(zero)]
-    before = [lax.rem(here + zero - s, zero) for s in range(zero)]
-    fetch = pltpu.make_async_copy(stored, weights, load)
-    fetch.start()
-    greet([], after[1:])
-
-    def columns_of(z):
-        return pl.ds(pl.multiple_of(z * owned, 128), owned)
-
-    coming = []
-    for s in range(1, zero):
-        copy = mate(rows.at[:, columns_of(after[s])], guest.at[s - 1], send.at[s, 0], recv.at[s, 0], after[s])
-        copy.start()
-        coming.append(copy)
-    edges = list(range(0, inner, 256)) + [inner]
-    spans = [(inner, exact)] + list(zip(edges[:-1], edges[1:]))
-    fetch.wait()
-    mine = rows[:, columns_of(here)]
-    for low, high in spans + [(exact, columns)]:
-        kept[:, low:high] = dot(mine, weights[low:high], ((1,), (1,)))
-    going = {}
-    narrow[...] = jnp.zeros(narrow.shape, F32)
-    for s in range(1, zero):
-        coming[s - 1].wait()
-        narrow[s - 1, :, :heads] = dot(guest[s - 1], weights[exact:], ((1,), (1,)))
-        copy = mate(narrow.at[s - 1], thin.at[s - 1], send.at[s, 1], recv.at[s, 1], before[s])
-        copy.start()
-        going[s, -1] = copy
-        for i, (low, high) in enumerate(spans):
-            value = dot(guest[s - 1], weights[low:high], ((1,), (1,)))
-            made[s - 1, :, low:high] = value.astype(BF)
-            copy = mate(
-                made.at[s - 1, :, low:high],
-                back.at[s - 1, :, low:high],
-                send.at[s, 2 + i],
-                recv.at[s, 2 + i],
-                before[s],
-            )
-            copy.start()
-            going[s, i] = copy
-    total = kept[:, exact:]
-    for s in range(1, zero):
-        going[s, -1].wait()
-        total = total + thin[s - 1, :, :heads]
-    raw[...] = total
-    for i, (low, high) in enumerate(spans):
-        total = kept[:, low:high]
-        for s in range(1, zero):
-            going[s, i].wait()
-            total = total + back[s - 1, :, low:high].astype(F32)
-        if i:
-            xs[:, low:high] = total.astype(BF)
-        else:
-            pair[...] = total.astype(BF)
-
-
-def head(rows, weights, inner, heads):
-    count, width = rows.shape
-    columns, owned = weights.shape
-    zero = width // owned
-    exact = columns - heads
-    steps = 3 + -(-inner // 256)
-    return pl.pallas_call(
-        functools.partial(head_kernel, zero, inner),
-        out_shape=(
-            jax.ShapeDtypeStruct((count, inner), BF),
-            jax.ShapeDtypeStruct((count, exact - inner), BF),
-            jax.ShapeDtypeStruct((count, heads), F32),
-        ),
-        in_specs=[pl.BlockSpec(memory_space=pltpu.VMEM), pl.BlockSpec(memory_space=pl.ANY)],
-        out_specs=[pl.BlockSpec(memory_space=pltpu.VMEM)] * 3,
-        scratch_shapes=[
-            pltpu.VMEM((columns, owned), BF),
-            pltpu.VMEM((zero - 1, count, owned), BF),
-            pltpu.VMEM((count, columns), F32),
-            pltpu.VMEM((zero - 1, count, exact), BF),
-            pltpu.VMEM((zero - 1, count, 128), F32),
-            pltpu.VMEM((zero - 1, count, exact), BF),
-            pltpu.VMEM((zero - 1, count, 128), F32),
-            pltpu.SemaphoreType.DMA((zero, steps)),
-            pltpu.SemaphoreType.DMA((zero, steps)),
-            pltpu.SemaphoreType.DMA,
-        ],
-        compiler_params=pltpu.CompilerParams(collective_id=2, vmem_limit_bytes=14 << 20, has_side_effects=True),
-    )(rows, weights)
-
-
 def core_kernel(
     width, chunk, lags, spans, tile,
-    xs, joined, raws, gy, rows, stored, a_log, dt_bias, d_skip, y_out, out, grads,
-    spread, dts, grows, fades, xds, growns, fadeds, ins, backs, cums, turned, mark, marks, gains,
+    rows, stored, gy, a_log, dt_bias, d_skip, y_out, out, grads,
+    xs, joined, guest, kept, shares, narrow, returned, thinned, hsend, hrecv, spread, dts, grows, fades, xds, growns, fadeds, ins, backs, cums, turned, mark, marks, gains,
     loc, both, pairs, duo, sums, far, ret, came, fin, wide, tall, left, right, weights, made,
     tsend, trecv, send, recv, zsend, zrecv, leave, enter, *scratch
 ):
@@ -164,13 +70,63 @@
     after = [lax.rem(here + s, zero) for s in range(zero)]
     before = [lax.rem(here + zero - s, zero) for s in range(zero)]
     count, inner = xs.shape
-    heads = raws.shape[1]
+    heads = a_log.shape[1]
+    columns, owned = weights.shape
+    exact = columns - heads
     size = joined.shape[1] // 2
     chunks = inner // chunk
     high = lax.Precision.HIGHEST
     far[...] = jnp.zeros(far.shape, BF)
     mark[...] = jnp.zeros(mark.shape, F32)
+    narrow[...] = jnp.zeros(narrow.shape, F32)
     greet(peers, after[1:])
+
+    def columns_of(z):
+        return pl.ds(pl.multiple_of(z * owned, 128), owned)
+
+    coming = []
+    for s in range(1, zero):
+        copy = mate(
+            rows.at[:, columns_of(after[s])],
+            guest.at[s - 1],
+            hsend.at[s, 0],
+            hrecv.at[s, 0],
+            after[s],
+        )
+        copy.start()
+        coming.append(copy)
+    step = min(256, chunk)
+    slabs = [(inner, exact)] + [(low, low + step) for low in range(0, inner, step)]
+    load.wait()
+    for low, top in slabs + [(exact, columns)]:
+        kept[:, low:top] = dot(rows[:, columns_of(here)], weights[low:top], ((1,), (1,)))
+    going = {}
+    for s in range(1, zero):
+        coming[s - 1].wait()
+        narrow[s - 1, :, :heads] = dot(guest[s - 1], weights[exact:], ((1,), (1,)))
+        going[s, -1] = mate(
+            narrow.at[s - 1], thinned.at[s - 1], hsend.at[s, 1], hrecv.at[s, 1], before[s]
+        )
+        going[s, -1].start()
+        for i, (low, top) in enumerate(slabs):
+            shares[s - 1, :, low:top] = dot(guest[s - 1], weights[low:top], ((1,), (1,))).astype(BF)
+            going[s, i] = mate(
+                shares.at[s - 1, :, low:top],
+                returned.at[s - 1, :, low:top],
+                hsend.at[s, 2 + i],
+                hrecv.at[s, 2 + i],
+                before[s],
+            )
+            going[s, i].start()
+
+    def slab(i):
+        low, top = slabs[i]
+        value = kept[:, low:top]
+        for s in range(1, zero):
+            going[s, i].wait()
+            value = value + returned[s - 1, :, low:top].astype(F32)
+        return value.astype(BF)
+
     def iota(shape, axis):
         return lax.broadcasted_iota(jnp.int32, shape, axis)
 
@@ -180,7 +136,11 @@
     lane = iota((heads, inner), 1)
     spread[...] = ((lane >= first) & (lane < first + width)).astype(F32)
     rate, skip = -jnp.exp(a_log[...]), d_skip[...]
-    raw = raws[...] + dt_bias[...]
+    raw = kept[:, exact:]
+    for s in range(1, zero):
+        going[s, -1].wait()
+        raw = raw + thinned[s - 1, :, :heads]
+    raw = raw + dt_bias[...]
     dt = jnp.maximum(raw, 0.0) + jnp.log1p(jnp.exp(-jnp.abs(raw)))
     cum = jnp.dot(ones, rate * dt, precision=high, preferred_element_type=F32)
     total = cum[count - 1 : count]
@@ -194,6 +154,7 @@
     for copy in told:
         copy.start()
     growth, fade = jnp.exp(cum), jnp.exp(total - cum)
+    joined[...] = slab(0)
     bm, cm = joined[:, :size], joined[:, size:]
     bt, ct = bm.T, cm.T
     skips = jnp.broadcast_to(skip, (8, heads))
@@ -207,13 +168,13 @@
             preferred_element_type=F32,
         )
 
-    step = min(256, chunk)
     copies = {}
 
     def prepare(c):
         for low in range(c * chunk, (c + 1) * chunk, step):
             top = low + step
             own = slice(low - c * chunk, low - c * chunk + step)
+            xs[:, low:top] = slab(1 + low // step)
             d, g, f = expand(dt, low, top), expand(growth, low, top), expand(fade, low, top)
             dts[:, low:top], grows[:, low:top], fades[:, low:top] = d, g, f
             xd = (xs[:, low:top].astype(F32) * d).astype(BF)
@@ -433,7 +394,6 @@
             copy.start()
             arriving[h].append(copy)
 
-    columns, owned = weights.shape
     mine_at = pl.multiple_of(here * owned, 128)
 
     def project(values, target, origin):
@@ -503,7 +463,6 @@
             join(k - 1)
             begin(k - 1, 0)
         if k == parts:
-            load.wait()
             for s in range(1, zero):
                 project(right.at[s * count : (s + 1) * count], made.at[s - 1], 0)
                 copy = mate(
@@ -526,14 +485,14 @@
                     low, high = spans[h][0], min(spans[h][1], columns)
                     out[:, low:high] = acc[h][chip, :, : high - low]
 
-    for c in range(chunks):
-        prepare(c)
-    for copy in told:
-        copy.wait()
-    totals = marks[:, 0, :heads]
-    for low in range(0, inner, step):
-        gains[:, low : low + step] = expand(totals, low, low + step)
-    stages = [stage_pair, stage_plane, stage_far, stage_back, finish]
+    def spread_totals():
+        for copy in told:
+            copy.wait()
+        totals = marks[:, 0, :heads]
+        for low in range(0, inner, step):
+            gains[:, low : low + step] = expand(totals, low, low + step)
+
+    stages = [prepare, stage_pair, stage_plane, stage_far, stage_back, finish]
     steps = chunks + lags[-1]
     fillers = list(range(inner // 128))
     per = -(-len(fillers) // lags[-1])
@@ -545,6 +504,8 @@
                 if stage is finish:
                     while fillers and fillers[0] * 128 < (c + 1) * chunk:
                         inside(fillers.pop(0))
+                if stage is stage_pair and c == 0:
+                    spread_totals()
                 stage(c)
                 if stage is finish:
                     for h in range(parts):
@@ -553,7 +514,7 @@
         if k == 0:
             cross()
         for _ in range(per):
-            if fillers:
+            if fillers and fillers[0] * 128 < (k + 1) * chunk:
                 inside(fillers.pop(0))
         if k == lags[-1] + 1:
             for copy in crossing:
@@ -584,11 +545,12 @@
         copy.wait()
 
 
-def ssd_block(xs, joined, raw, gy, rows, weights, a_log, dt_bias, d_skip):
+def layer(rows, weights, gy, a_log, dt_bias, d_skip):
     count, inner = gy.shape
     heads = a_log.shape[0]
-    size = joined.shape[1] // 2
     columns, owned = weights.shape
+    exact = columns - heads
+    size = (exact - inner) // 2
     seq, zero = lax.axis_size("seq"), lax.axis_size("zero")
     planes, pieces = seq // 4, seq // 2
     piece, tokens = owned // seq, zero * count
@@ -606,7 +568,18 @@
     block = pltpu.VMEM((chunks, 2, 2, 2, quarter, chunk), BF)
     half = pltpu.VMEM((chunks, 2, 2, quarter, chunk), BF)
     dma = pltpu.SemaphoreType.DMA
+    slabs = 3 + -(-inner // 256)
     scratch = [
+        thin,
+        pltpu.VMEM((count, 2 * size), BF),
+        pltpu.VMEM((zero - 1, count, owned), BF),
+        pltpu.VMEM((count, columns), F32),
+        pltpu.VMEM((zero - 1, count, exact), BF),
+        pltpu.VMEM((zero - 1, count, 128), F32),
+        pltpu.VMEM((zero - 1, count, exact), BF),
+        pltpu.VMEM((zero - 1, count, 128), F32),
+        dma((zero, slabs)),
+        dma((zero, slabs)),
         pltpu.VMEM((heads, inner), F32),
         tall, tall, tall, thin, thin, thin, tall, tall,
         pltpu.VMEM((count, heads), F32),
@@ -643,24 +616,20 @@
             jax.ShapeDtypeStruct((piece, columns), F32),
             jax.ShapeDtypeStruct((count, zero * owned), BF),
         ),
-        in_specs=[local] * 5 + [pl.BlockSpec(memory_space=pl.ANY)] + [local] * 3,
+        in_specs=[local, pl.BlockSpec(memory_space=pl.ANY)] + [local] * 4,
         out_specs=[local] * 3,
         scratch_shapes=scratch,
-        compiler_params=pltpu.CompilerParams(collective_id=0, vmem_limit_bytes=48 << 20, has_side_effects=True),
-    )(xs, joined, raw, gy, rows, weights, a_log[None], dt_bias[None], d_skip[None])
+        compiler_params=pltpu.CompilerParams(collective_id=0, vmem_limit_bytes=VMEM, has_side_effects=True),
+    )(rows, weights, gy, a_log[None], dt_bias[None], d_skip[None])
 
 
 def per_device(tokens, w_in, a_log, dt_bias, d_skip, grad_y):
     count, width = tokens.shape[1:]
     inner = grad_y.shape[2]
-    heads = a_log.shape[0]
     rows = tokens.reshape(count, width)
 
-    stored = w_in.T
-    xs, joined, raw = head(rows, stored, inner, heads)
-
-    y_out, grad_w, grad_tokens = ssd_block(
-        xs, joined, raw, grad_y.reshape(count, inner), rows, stored, a_log, dt_bias, d_skip
+    y_out, grad_w, grad_tokens = layer(
+        rows, w_in.T, grad_y.reshape(count, inner), a_log, dt_bias, d_skip
     )
     grad_tokens = grad_tokens.reshape(1, count, width)
     return (y_out.reshape(1, count, inner), grad_tokens, grad_w)

time: 100 us -> 89.7 us (0.90)
  Pallas kernels: 93.7 us -> 83.1 us
    pallas_call x2 -> x1, Pallas kernels: 93.7 us -> 83.1 us  [layer(): pl.pallas_call(functools.partial(core_kernel, inner // heads, chunk, LAGS...]
    unnamed x17 -> x3, local copies, waits for them, and re-layouts: 5.84 us -> 5.7 us
where the time goes in v1:
time: 89.7 us; the launch traced here: 89.4 us
  Pallas kernels  83.1 us (93%)
  local copies, waits for them, and re-layouts  5.7 us (6%)
    pallas_call x1, Pallas kernels, layer(): pl.pallas_call(functools.partial(core_kernel, inner // heads, chunk, LAGS...  83.1 us
    unnamed x3, local copies, waits for them, and re-layouts  5.7 us

profile of v1, /device:TPU:0, one launch (start us, length us, event | category | flops | bytes accessed | tf_op | source)
XLA Modules:
  0.0 89.4 jit_solution(6614950107618631856)
XLA Ops:
  0.6 83.1 %shard_map.85 = (bf16[128,2048]{1,0:T(8,128)(2,1)}, f32[64,2336]{1,0:T(8,128)}, bf16[128,2048]{1,0:T(8,128)(2,1)}) custom-call(bf16[128,2048]{1,0:T(8,128)(2,1)} %bitcast.9, bf16[2336,1024]{1,0:T(8,128)(2,1)} %bitcast.8, bf16[128,2048]{1,0:T(8,128)(2,1)} %bitcast.10, f32[1,32]{1,0:T(1,128)} %bitcast.13, f32[1,32]{1,0:T(1,128)} %bitcast.14, f32[1,32]{1,0:T(1,128)} %bitcast.15), custom_call_target="tpu_custom_call" | custom-call | tf_op jit(solution)/shard_map/pallas_call | solution.py:612
  83.7 1.9 %copy.12 = bf16[1,128,2048]{2,1,0:T(8,128)(2,1)} copy(bf16[1,128,2048]{2,1,0:T(8,128)(2,1)} %bitcast.12) | data formatting | bytes 1048576
  85.6 1.9 %copy.13 = bf16[1,128,2048]{2,1,0:T(8,128)(2,1)} copy(bf16[1,128,2048]{2,1,0:T(8,128)(2,1)} %bitcast.11) | data formatting | bytes 1048576
  87.5 1.9 %copy.14 = f32[64,2336]{1,0:T(8,128)} copy(f32[64,2336]{1,0:T(8,128)} %get-tuple-element.14) | data formatting | bytes 1196032

commit v2 on v1

--- a/solution.py
+++ b/solution.py
@@ -8,7 +8,7 @@
 from jax.sharding import PartitionSpec as P
 
 BF = jnp.bfloat16
-VMEM = 56 << 20
+VMEM = 50 << 20
 F32 = jnp.float32
 MESH = pl.DeviceIdType.MESH
 LAGS = (0, 1, 2, 4, 5, 6)

time: 89.7 us -> 88 us (0.981)
  Pallas kernels: 83.1 us -> 80.7 us
    pallas_call x1, Pallas kernels: 83.1 us -> 80.7 us  [layer(): pl.pallas_call(functools.partial(core_kernel, inner // heads, chunk, LAGS...]
    unnamed x3 -> x13, local copies, waits for them, and re-layouts: 5.7 us -> 6.45 us
where the time goes in v2:
time: 88 us; the launch traced here: 87.8 us
  Pallas kernels  80.7 us (92%)
  local copies, waits for them, and re-layouts  6.45 us (7%)
    pallas_call x1, Pallas kernels, layer(): pl.pallas_call(functools.partial(core_kernel, inner // heads, chunk, LAGS...  80.7 us
    unnamed x13, local copies, waits for them, and re-layouts  6.45 us

profile of v2, /device:TPU:0, one launch (start us, length us, event | category | flops | bytes accessed | tf_op | source)
XLA Modules:
  0.0 87.8 jit_solution(9228498012511556528)
XLA Ops:
  0.6 0.0 copy-start
  0.6 1.0 %copy-done = bf16[1,128,2048]{2,1,0:T(8,128)(2,1)S(1)} copy-done((bf16[1,128,2048]{2,1,0:T(8,128)(2,1)S(1)}, bf16[1,128,2048]{2,1,0:T(8,128)(2,1)}, u32[]{:S(2)}) %copy-start) | copy-done | bytes 524312
  1.7 0.0 copy-start.1
  1.7 1.0 %copy-done.1 = bf16[1,128,2048]{2,1,0:T(8,128)(2,1)S(1)} copy-done((bf16[1,128,2048]{2,1,0:T(8,128)(2,1)S(1)}, bf16[1,128,2048]{2,1,0:T(8,128)(2,1)}, u32[]{:S(2)}) %copy-start.1) | copy-done | bytes 524312
  2.7 0.0 copy-start.2
  2.7 0.7 copy-done.2
  3.4 0.0 copy-start.3
  3.4 0.7 copy-done.3
  4.0 0.0 copy-start.4
  4.0 0.7 copy-done.4
  4.7 80.7 %shard_map.85 = (bf16[128,2048]{1,0:T(8,128)(2,1)S(1)}, f32[64,2336]{1,0:T(8,128)S(1)}, bf16[128,2048]{1,0:T(8,128)(2,1)S(1)}) custom-call(bf16[128,2048]{1,0:T(8,128)(2,1)S(1)} %bitcast.8, bf16[2336,1024]{1,0:T(8,128)(2,1)} %bitcast.15, bf16[128,2048]{1,0:T(8,128)(2,1)S(1)} %bitcast.9, f32[1,32]{1,0:T(1,128)S(1)} %bitcast.12, f32[1,32]{1,0:T(1,128)S(1)} %bitcast.13, ...), custom_call_target="tpu_custom_call" | custom-call | tf_op jit(solution)/shard_map/pallas_call | solution.py:612
  85.4 0.8 copy.12
  86.2 0.8 copy.13
  86.9 0.8 copy.14
Async XLA Ops:
  0.6 1.0 %copy-start = (bf16[1,128,2048]{2,1,0:T(8,128)(2,1)S(1)}, bf16[1,128,2048]{2,1,0:T(8,128)(2,1)}, u32[]{:S(2)}) copy-start(bf16[1,128,2048]{2,1,0:T(8,128)(2,1)} %param.6) | copy-start | bytes 1572868
  1.7 1.0 %copy-start.1 = (bf16[1,128,2048]{2,1,0:T(8,128)(2,1)S(1)}, bf16[1,128,2048]{2,1,0:T(8,128)(2,1)}, u32[]{:S(2)}) copy-start(bf16[1,128,2048]{2,1,0:T(8,128)(2,1)} %param.11) | copy-start | bytes 1572868
  2.7 0.7 copy-start.2
  3.4 0.7 copy-start.3
  4.0 0.7 copy-start.4

commit v3 on v2

--- a/solution.py
+++ b/solution.py
@@ -12,7 +12,7 @@
 F32 = jnp.float32
 MESH = pl.DeviceIdType.MESH
 LAGS = (0, 1, 2, 4, 5, 6)
-SPACING = (3, 3)
+SPACING = (3, 4)
 SWAPPED = (0, 5)
 
 
@@ -53,14 +53,22 @@
 
 def core_kernel(
     width, chunk, lags, spans, tile,
-    rows, stored, gy, a_log, dt_bias, d_skip, y_out, out, grads,
-    xs, joined, guest, kept, shares, narrow, returned, thinned, hsend, hrecv, spread, dts, grows, fades, xds, growns, fadeds, ins, backs, cums, turned, mark, marks, gains,
+    far_rows, stored, far_gy, far_a, far_bias, far_skip, y_out, out, grads,
+    rows, gy, a_log, dt_bias, d_skip, fetched, xs, joined, guest, kept, shares, narrow, returned, thinned, hsend, hrecv, spread, dts, grows, fades, xds, growns, fadeds, ins, backs, cums, turned, mark, marks, gains,
     loc, both, pairs, duo, sums, far, ret, came, fin, wide, tall, left, right, weights, made,
     tsend, trecv, send, recv, zsend, zrecv, leave, enter, *scratch
 ):
     seq, planes = marks.shape[0], far.shape[2]
     zero = tall.shape[2]
     load = pltpu.make_async_copy(stored, weights, scratch[-1])
+    fetches = [
+        pltpu.make_async_copy(source, target, fetched.at[i])
+        for i, (source, target) in enumerate(
+            [(far_rows, rows), (far_gy, gy), (far_a, a_log), (far_bias, dt_bias), (far_skip, d_skip)]
+        )
+    ]
+    for copy in fetches:
+        copy.start()
     load.start()
     me, here = lax.axis_index("seq"), lax.axis_index("zero")
     core, chip = lax.rem(me, 2), lax.div(me, 2)
@@ -80,6 +88,8 @@
     mark[...] = jnp.zeros(mark.shape, F32)
     narrow[...] = jnp.zeros(narrow.shape, F32)
     greet(peers, after[1:])
+    for copy in fetches:
+        copy.wait()
 
     def columns_of(z):
         return pl.ds(pl.multiple_of(z * owned, 128), owned)
@@ -569,7 +579,14 @@
     half = pltpu.VMEM((chunks, 2, 2, quarter, chunk), BF)
     dma = pltpu.SemaphoreType.DMA
     slabs = 3 + -(-inner // 256)
+    scalar = pltpu.VMEM((1, heads), F32)
     scratch = [
+        pltpu.VMEM(rows.shape, BF),
+        thin,
+        scalar,
+        scalar,
+        scalar,
+        dma((5,)),
         thin,
         pltpu.VMEM((count, 2 * size), BF),
         pltpu.VMEM((zero - 1, count, owned), BF),
@@ -616,7 +633,7 @@
             jax.ShapeDtypeStruct((piece, columns), F32),
             jax.ShapeDtypeStruct((count, zero * owned), BF),
         ),
-        in_specs=[local, pl.BlockSpec(memory_space=pl.ANY)] + [local] * 4,
+        in_specs=[pl.BlockSpec(memory_space=pltpu.HBM)] * 6,
         out_specs=[local] * 3,
         scratch_shapes=scratch,
         compiler_params=pltpu.CompilerParams(collective_id=0, vmem_limit_bytes=VMEM, has_side_effects=True),

time: 88 us -> 86.9 us (0.988)
  Pallas kernels: 80.7 us -> 79.5 us
    pallas_call x1, Pallas kernels: 80.7 us -> 79.5 us  [layer(): pl.pallas_call(functools.partial(core_kernel, inner // heads, chunk, LAGS...]
where the time goes in v3:
time: 86.9 us; the launch traced here: 86.6 us
  Pallas kernels  79.5 us (91%)
  local copies, waits for them, and re-layouts  6.45 us (7%)
    pallas_call x1, Pallas kernels, layer(): pl.pallas_call(functools.partial(core_kernel, inner // heads, chunk, LAGS...  79.5 us
    unnamed x13, local copies, waits for them, and re-layouts  6.45 us

profile of v3, /device:TPU:0, one launch (start us, length us, event | category | flops | bytes accessed | tf_op | source)
XLA Modules:
  0.0 86.6 jit_solution(2682529587372423901)
XLA Ops:
  0.6 0.0 copy-start
  0.6 1.0 %copy-done = bf16[1,128,2048]{2,1,0:T(8,128)(2,1)S(1)} copy-done((bf16[1,128,2048]{2,1,0:T(8,128)(2,1)S(1)}, bf16[1,128,2048]{2,1,0:T(8,128)(2,1)}, u32[]{:S(2)}) %copy-start) | copy-done | bytes 524312
  1.7 0.0 copy-start.1
  1.7 1.0 %copy-done.1 = bf16[1,128,2048]{2,1,0:T(8,128)(2,1)S(1)} copy-done((bf16[1,128,2048]{2,1,0:T(8,128)(2,1)S(1)}, bf16[1,128,2048]{2,1,0:T(8,128)(2,1)}, u32[]{:S(2)}) %copy-start.1) | copy-done | bytes 524312
  2.7 0.0 copy-start.2
  2.7 0.7 copy-done.2
  3.4 0.0 copy-start.3
  3.4 0.7 copy-done.3
  4.0 0.0 copy-start.4
  4.0 0.7 copy-done.4
  4.7 79.5 %shard_map.85 = (bf16[128,2048]{1,0:T(8,128)(2,1)S(1)}, f32[64,2336]{1,0:T(8,128)S(1)}, bf16[128,2048]{1,0:T(8,128)(2,1)S(1)}) custom-call(bf16[128,2048]{1,0:T(8,128)(2,1)S(1)} %bitcast.8, bf16[2336,1024]{1,0:T(8,128)(2,1)} %bitcast.15, bf16[128,2048]{1,0:T(8,128)(2,1)S(1)} %bitcast.9, f32[1,32]{1,0:T(1,128)S(1)} %bitcast.12, f32[1,32]{1,0:T(1,128)S(1)} %bitcast.13, ...), custom_call_target="tpu_custom_call" | custom-call | tf_op jit(solution)/shard_map/pallas_call | solution.py:629
  84.2 0.8 copy.12
  85.0 0.8 copy.13
  85.8 0.8 copy.14
Async XLA Ops:
  0.6 1.0 %copy-start = (bf16[1,128,2048]{2,1,0:T(8,128)(2,1)S(1)}, bf16[1,128,2048]{2,1,0:T(8,128)(2,1)}, u32[]{:S(2)}) copy-start(bf16[1,128,2048]{2,1,0:T(8,128)(2,1)} %param.6) | copy-start | bytes 1572868
  1.7 1.0 %copy-start.1 = (bf16[1,128,2048]{2,1,0:T(8,128)(2,1)S(1)}, bf16[1,128,2048]{2,1,0:T(8,128)(2,1)}, u32[]{:S(2)}) copy-start(bf16[1,128,2048]{2,1,0:T(8,128)(2,1)} %param.11) | copy-start | bytes 1572868
  2.7 0.7 copy-start.2
  3.4 0.7 copy-start.3
  4.0 0.7 copy-start.4
